TPU v7x, 128 devices: a whole 4x4x4 slice. The times are simulated.
128 devices in a mesh: seq: 32 (over z, x, y_hi), tp: 4 (over y_lo, core).
Axes of the slice: x: 4, y: 4 (y_hi: 2, y_lo: 2; y = y_hi * 2 + y_lo), z: 4, core: 2. Of those that a mesh axis runs over, the one named last changes fastest.
Arguments:
- queries: bfloat16 [65536, 2048], P('seq', 'tp'), may hold values from -6 to 6
- key_vectors: bfloat16 [65536, 2048], P('seq', 'tp'), may hold values from -6 to 6
- value_vectors: bfloat16 [65536, 2048], P('seq', 'tp'), may hold values from -6 to 6
- out_grad: bfloat16 [65536, 2048], P('seq', 'tp'), may hold values from -0.25 to 0.25
- log_decay: float32 [8, 65536], P(None, 'seq'), may hold values from -2 to 0, as said below
- inputs: bfloat16 [65536, 2048], P('seq'), may hold values from -0.109375 to 0.109375
Outputs:
- key_grad: bfloat16 [65536, 2048], P('seq', 'tp')
- value_grad: bfloat16 [65536, 2048], P('seq', 'tp')
- weight_grad: bfloat16 [2048, 2, 2048], P('seq', None, 'tp')
Inputs may be any that keep to these rules, and one draw needn't show every extreme that they name: `log_decay`: every entry is negative.
All inputs are finite; a program needn't handle non-finite values.
Results may differ from a plain program's by a relative error of at most 0.0066.
Values may be sent and summed in bfloat16 or wider, within the bound.
No kernel may reach another device: no remote copies, remote signals or barrier semaphores. Data moves between devices by JAX's collectives and lax.ppermute only.
A program may use at most 128 MiB of HBM per device.

v0:
```python
import functools

import jax
import jax.numpy as jnp
from jax import lax
from jax.experimental import pallas as pl
from jax.experimental.pallas import tpu as pltpu
from jax.sharding import Mesh
from jax.sharding import PartitionSpec as P

DH = 256
BLOCK = 512
SEQ = ("z", "x", "y")
TP = ("lo", "core")
EVERY = SEQ + TP
F32 = jnp.float32
BF16 = jnp.bfloat16
SCALE = DH ** (-0.5)


def cumulate(rows):
    lane = lax.broadcasted_iota(jnp.int32, rows.shape, 1)
    step = 1
    while step < rows.shape[1]:
        rows = rows + jnp.where(lane >= step, pltpu.roll(rows, step, 1), 0.0)
        step *= 2
    return rows


def own_rows(rows, first, heads):
    index = lax.broadcasted_iota(jnp.int32, rows.shape, 0)
    picked = [jnp.sum(jnp.where(index == first + h, rows, 0.0), axis=0, keepdims=True) for h in range(heads)]
    out = jnp.zeros_like(rows)
    for h in range(heads):
        out = jnp.where(index == h, picked[h], out)
    return out


def dot_tt(a, b):
    return lax.dot_general(a, b, (((0,), (0,)), ((), ())), preferred_element_type=F32)


def dot_nt(a, b):
    return lax.dot_general(a, b, (((1,), (1,)), ((), ())), preferred_element_type=F32)


def dot_nn(a, b):
    return jnp.dot(a, b, preferred_element_type=F32)


def states_kernel(heads, where_ref, q_ref, g_ref, ld_ref, state_ref, message_ref, total, passed):
    block = pl.program_id(0)

    @pl.when(block == 0)
    def _():
        total[...] = jnp.zeros_like(total)
        passed[...] = jnp.zeros_like(passed)

    cum = cumulate(own_rows(ld_ref[...], where_ref[0] * heads, heads))
    decay = (SCALE * jnp.exp(cum)).T
    for h in range(heads):
        cols = slice(h * DH, (h + 1) * DH)
        weighted = (q_ref[:, cols].astype(F32) * decay[:, h : h + 1]).astype(BF16)
        state = dot_tt(weighted, g_ref[:, cols])
        state_ref[0, h] = state
        total[h] = total[h] + jnp.exp(passed[h : h + 1, 0:1]) * state
    passed[...] = passed[...] + cum[:, BLOCK - 1 : BLOCK]

    @pl.when(block == pl.num_programs(0) - 1)
    def _():
        piece = message_ref.shape[1]
        each = DH // piece
        row = lax.broadcasted_iota(jnp.int32, (piece, 128), 0)
        for h in range(heads):
            gone = jnp.broadcast_to(passed[h : h + 1, :], (piece, 128))
            high = gone.astype(BF16).astype(F32)
            middle = (gone - high).astype(BF16).astype(F32)
            low = gone - high - middle
            tail = jnp.where(row == 0, high, jnp.where(row == 1, middle, jnp.where(row == 2, low, 0.0)))
            tail = tail.astype(BF16)
            for k in range(each):
                message_ref[h * each + k, :, :DH] = total[h, k * piece : (k + 1) * piece, :].astype(BF16)
                message_ref[h * each + k, :, DH:] = tail


def block_states(place, queries, out_grad, log_decay, devices):
    rows, width = queries.shape
    heads = width // DH
    blocks = rows // BLOCK
    piece = heads * DH // devices
    return pl.pallas_call(
        functools.partial(states_kernel, heads),
        grid_spec=pltpu.PrefetchScalarGridSpec(
            num_scalar_prefetch=1,
            grid=(blocks,),
            in_specs=[
                pl.BlockSpec((BLOCK, width), lambda i, s: (i, 0)),
                pl.BlockSpec((BLOCK, width), lambda i, s: (i, 0)),
                pl.BlockSpec((log_decay.shape[0], BLOCK), lambda i, s: (0, i)),
            ],
            out_specs=[
                pl.BlockSpec((1, heads, DH, DH), lambda i, s: (i, 0, 0, 0)),
                pl.BlockSpec((devices, piece, DH + 128), lambda i, s: (0, 0, 0)),
            ],
            scratch_shapes=[pltpu.VMEM((heads, DH, DH), F32), pltpu.VMEM((log_decay.shape[0], 128), F32)],
        ),
        out_shape=[
            jax.ShapeDtypeStruct((blocks, heads, DH, DH), F32),
            jax.ShapeDtypeStruct((devices, piece, DH + 128), BF16),
        ],
        cost_estimate=pl.CostEstimate(
            flops=2 * rows * width * DH, bytes_accessed=4 * rows * width + 4 * blocks * width * DH, transcendentals=rows
        ),
        name="states",
    )(place, queries, out_grad, log_decay)


def chain_kernel(message_ref, out_ref):
    devices, piece, _ = message_ref.shape
    carried = jnp.zeros((piece, DH), F32)
    for d in reversed(range(devices)):
        out_ref[d] = carried.astype(BF16)
        logs = jnp.sum(message_ref[d, :, DH:].astype(F32), axis=0, keepdims=True)
        gamma = jnp.exp(logs)
        gamma = jnp.concatenate([gamma] * (DH // 128), axis=1)
        carried = message_ref[d, :, :DH].astype(F32) + gamma * carried


def chain(message):
    devices, piece, _ = message.shape
    return pl.pallas_call(
        chain_kernel,
        out_shape=jax.ShapeDtypeStruct((devices, piece, DH), BF16),
        cost_estimate=pl.CostEstimate(flops=4 * devices * piece * DH, bytes_accessed=4 * message.size, transcendentals=0),
        name="chain",
    )(message)


def inside_kernel(heads, head, where_ref, q_ref, k_ref, v_ref, g_ref, ld_ref, ik_ref, iv_ref):
    cum = cumulate(own_rows(ld_ref[...], where_ref[0] * heads, heads))
    columns = cum.T
    half = BLOCK // 2
    row = lax.broadcasted_iota(jnp.int32, (half, half), 0)
    column = lax.broadcasted_iota(jnp.int32, (half, half), 1)
    seen = row >= column
    for j in range(2):
        sources = slice(j * half, (j + 1) * half)
        k, v = (k_ref[sources, :], v_ref[sources, :])
        key_part = value_part = None
        for i in range(j, 2):
            targets = slice(i * half, (i + 1) * half)
            q, g = (q_ref[targets, :], g_ref[targets, :])
            spread = columns[targets, head : head + 1] - cum[head : head + 1, sources]
            weights = SCALE * jnp.exp(jnp.minimum(spread, 0.0))
            if i == j:
                weights = jnp.where(seen, weights, 0.0)
            key_scores = (dot_nt(q, k) * weights).astype(BF16)
            grad_scores = (dot_nt(g, v) * weights).astype(BF16)
            to_key, to_value = (dot_tt(grad_scores, q), dot_tt(key_scores, g))
            key_part = to_key if key_part is None else key_part + to_key
            value_part = to_value if value_part is None else value_part + to_value
        ik_ref[sources, :] = key_part
        iv_ref[sources, :] = value_part


def inside(place, head, queries, keys, values, out_grad, log_decay):
    rows, width = queries.shape
    heads = width // DH
    tokens = pl.BlockSpec((BLOCK, DH), lambda i, s: (i, head))
    return pl.pallas_call(
        functools.partial(inside_kernel, heads, head),
        grid_spec=pltpu.PrefetchScalarGridSpec(
            num_scalar_prefetch=1,
            grid=(rows // BLOCK,),
            in_specs=[tokens] * 4 + [pl.BlockSpec((log_decay.shape[0], BLOCK), lambda i, s: (0, i))],
            out_specs=[pl.BlockSpec((BLOCK, DH), lambda i, s: (i, 0))] * 2,
        ),
        out_shape=[jax.ShapeDtypeStruct((rows, DH), F32)] * 2,
        cost_estimate=pl.CostEstimate(
            flops=8 * rows * DH * BLOCK, bytes_accessed=16 * rows * DH, transcendentals=rows * BLOCK
        ),
        name=f"inside{head}",
    )(place, queries, keys, values, out_grad, log_decay)


def finish_kernel(heads, blocks, where_ref, c_ref, state_ref, k_ref, v_ref, ld_ref, *refs):
    inner = refs[: 2 * heads]
    x_ref, kg_ref, vg_ref, out_ref, carry, grads = refs[2 * heads :]
    step = pl.program_id(0)
    width = heads * DH

    @pl.when(step == 0)
    def _():
        carry[...] = c_ref[...].astype(F32)

    @pl.when(step < blocks)
    def _():
        cum = cumulate(own_rows(ld_ref[...], where_ref[0] * heads, heads))
        last = cum[:, BLOCK - 1 : BLOCK]
        decayed = jnp.exp(last - cum).T
        rows = pl.ds(pl.multiple_of((blocks - 1 - step) * BLOCK, BLOCK), BLOCK)
        for h in range(heads):
            cols = slice(h * DH, (h + 1) * DH)
            low = carry[h].astype(BF16)
            over = decayed[:, h : h + 1]
            key_grad = (inner[2 * h][...] + over * dot_nt(v_ref[:, cols], low)).astype(BF16)
            value_grad = (inner[2 * h + 1][...] + over * dot_nn(k_ref[:, cols], low)).astype(BF16)
            kg_ref[:, cols] = key_grad
            vg_ref[:, cols] = value_grad
            grads[rows, cols] = key_grad
            grads[rows, width + h * DH : width + (h + 1) * DH] = value_grad
            carry[h] = jnp.exp(last[h : h + 1, :]) * carry[h] + state_ref[0, h]

    @pl.when(step >= blocks)
    def _():
        devices, share, lanes = out_ref.shape
        strips = 2 * width // lanes
        share = share // strips
        for part in range(2):
            sums = dot_tt(x_ref[...], grads[:, part * width : (part + 1) * width]).astype(BF16)
            for d in range(devices):
                for c in range(width // lanes):
                    at = (part * (width // lanes) + c) * share
                    out_ref[d, at : at + share, :] = sums[d * share : (d + 1) * share, c * lanes : (c + 1) * lanes]


def finish(place, carried, states, keys, values, log_decay, inner, inputs, devices):
    rows, width = keys.shape
    heads = width // DH
    blocks = rows // BLOCK
    steps = 4
    wide = inputs.shape[1]
    share = wide // devices

    def back(i):
        return jnp.maximum(blocks - 1 - i, 0)

    def later(i):
        return jnp.maximum(i - blocks, 0)

    tokens = pl.BlockSpec((BLOCK, width), lambda i, s: (back(i), 0))
    return pl.pallas_call(
        functools.partial(finish_kernel, heads, blocks),
        grid_spec=pltpu.PrefetchScalarGridSpec(
            num_scalar_prefetch=1,
            grid=(blocks + steps,),
            in_specs=[
                pl.BlockSpec((heads, DH, DH), lambda i, s: (0, 0, 0)),
                pl.BlockSpec((1, heads, DH, DH), lambda i, s: (back(i), 0, 0, 0)),
                tokens,
                tokens,
                pl.BlockSpec((log_decay.shape[0], BLOCK), lambda i, s: (0, back(i))),
            ]
            + [pl.BlockSpec((BLOCK, DH), lambda i, s: (back(i), 0))] * (2 * heads)
            + [pl.BlockSpec((rows, wide // steps), lambda i, s: (0, later(i)))],
            out_specs=[
                tokens,
                tokens,
                pl.BlockSpec((devices // steps, 2 * share * width // 128, 128), lambda i, s: (later(i), 0, 0)),
            ],
            scratch_shapes=[pltpu.VMEM((heads, DH, DH), F32), pltpu.VMEM((rows, 2 * width), BF16)],
        ),
        out_shape=[jax.ShapeDtypeStruct((rows, width), BF16)] * 2
        + [pltpu.VMEM((devices, 2 * share * width // 128, 128), BF16)],
        cost_estimate=pl.CostEstimate(
            flops=4 * rows * width * (DH + wide), bytes_accessed=16 * rows * width, transcendentals=rows * heads
        ),
        compiler_params=pltpu.CompilerParams(vmem_limit_bytes=48 << 20),
        name="finish",
    )(place, carried, states, keys, values, log_decay, *inner, inputs)


def gather_kernel(parts_ref, out_ref):
    devices, rows, lanes = parts_ref.shape
    share, _, width = out_ref.shape
    strips = width // lanes
    step = 32
    for start in range(0, rows, step):
        total = parts_ref[0, start : start + step, :].astype(F32)
        for d in range(1, devices):
            total = total + parts_ref[d, start : start + step, :].astype(F32)
        part, strip = divmod(start // share, strips)
        at = start % share
        out_ref[at : at + step, part, strip * lanes : (strip + 1) * lanes] = total.astype(BF16)


def gathered(parts, width):
    rows = parts.shape[1] * parts.shape[2] // width
    return pl.pallas_call(
        gather_kernel,
        in_specs=[pl.BlockSpec(memory_space=pltpu.VMEM)],
        out_shape=jax.ShapeDtypeStruct((rows // 2, 2, width), BF16),
        cost_estimate=pl.CostEstimate(flops=parts.size, bytes_accessed=2 * parts.size, transcendentals=0),
        compiler_params=pltpu.CompilerParams(vmem_limit_bytes=12 << 20),
        name="gathered",
    )(parts)


def shards(queries, keys, values, out_grad, log_decay, inputs):
    devices = lax.axis_size(SEQ)
    width = queries.shape[1]
    place = lax.axis_index(TP).astype(jnp.int32).reshape(1)
    states, message = block_states(place, queries, out_grad, log_decay, devices)
    tokens = (queries, keys, values, out_grad, log_decay)
    arrived = lax.all_to_all(message, SEQ, 0, 0, tiled=True)
    inner = list(inside(place, 0, *tokens))
    arrived, place, *inner = lax.optimization_barrier((arrived, place, *inner))
    carried = lax.all_to_all(chain(arrived), SEQ, 0, 0, tiled=True)
    inner += inside(place, 1, *tokens)
    key_grad, value_grad, parts = finish(
        place, carried.reshape(-1, DH, DH), states, keys, values, log_decay, inner, inputs, devices
    )
    parts = lax.all_to_all(parts, SEQ, 0, 0, tiled=True)
    return (key_grad, value_grad, gathered(parts, width))


def solution(mesh):
    split = Mesh(mesh.devices.reshape(4, 4, 2, 2, 2), EVERY)
    placed = (P(SEQ, TP),) * 4 + (P(None, SEQ), P(SEQ, None))
    return jax.shard_map(
        shards,
        mesh=split,
        in_specs=placed,
        out_specs=(P(SEQ, TP), P(SEQ, TP), P(SEQ, None, TP)),
        check_vma=False,
    )
```

profile of v0, /device:TPU:1, one launch (start us, length us, event | category | flops | bytes accessed | tf_op | source)
XLA Modules:
  0.0 129.3 jit_solution(13610345673496533883)
XLA Ops:
  0.6 7.3 %states.1 = (f32[4,2,256,256]{3,2,1,0:T(8,128)}, bf16[32,16,384]{2,1,0:T(8,128)(2,1)}) custom-call(s32[1]{0:T(128)} %bitcast.where_ref, bf16[2048,512]{1,0:T(8,128)(2,1)} %q_ref.5, bf16[2048,512]{1,0:T(8,128)(2,1)} %g_ref.5, f32[8,2048]{1,0:T(8,128)} %ld_ref.7), custom_call_target="tpu_custom_call" | custom-call | flops 536870912 | bytes 6291456 | tf_op jit(solution)/shard_map/states/pallas_call | solution.py:91
  7.9 11.3 %all-to-all-start = ((bf16[32,16,384]{2,1,0:T(8,128)(2,1)}), bf16[32,16,384]{2,1,0:T(8,128)(2,1)S(1)}, u32[]{:S(2)}, u32[]{:S(2)}) async-start(bf16[32,16,384]{2,1,0:T(8,128)(2,1)} %get-tuple-element.16), calls=%async_computation | async-start | bytes 786432 | tf_op jit(solution)/shard_map/all_to_all | solution.py:305
  19.3 8.5 %inside0.1 = (f32[2048,256]{1,0:T(8,128)}, f32[2048,256]{1,0:T(8,128)}) custom-call(s32[1]{0:T(128)} %bitcast.where_ref, bf16[2048,512]{1,0:T(8,128)(2,1)} %q_ref.5, bf16[2048,512]{1,0:T(8,128)(2,1)} %k_ref.5, bf16[2048,512]{1,0:T(8,128)(2,1)} %v_ref.5, bf16[2048,512]{1,0:T(8,128)(2,1)} %g_ref.5, f32[8,2048]{1,0:T(8,128)} %ld_ref.7), custom_call_target="tpu_custom_call" | custom-call | flops 2147483648 | bytes 8388608 | tf_op jit(solution)/shard_map/inside0/pallas_call | solution.py:170
  27.8 3.0 %all-to-all-done.message_ref = bf16[32,16,384]{2,1,0:T(8,128)(2,1)S(1)} async-done(((bf16[32,16,384]{2,1,0:T(8,128)(2,1)}), bf16[32,16,384]{2,1,0:T(8,128)(2,1)S(1)}, u32[]{:S(2)}, u32[]{:S(2)}) %all-to-all-start) | async-done | bytes 393248 | tf_op jit(solution)/shard_map/all_to_all | solution.py:305
  30.8 0.0 copy-start.1
  30.8 0.7 copy-done.1
  31.5 1.8 %chain.1 = bf16[32,16,256]{2,1,0:T(8,128)(2,1)} custom-call(bf16[32,16,384]{2,1,0:T(8,128)(2,1)} %copy-done.1), custom_call_target="tpu_custom_call" | custom-call | flops 524288 | bytes 786432 | tf_op jit(solution)/shard_map/chain/pallas_call | solution.py:131
  33.3 6.3 %all-to-all-start.1 = ((bf16[32,16,256]{2,1,0:T(8,128)(2,1)}), bf16[32,16,256]{2,1,0:T(8,128)(2,1)S(1)}, u32[]{:S(2)}, u32[]{:S(2)}) async-start(bf16[32,16,256]{2,1,0:T(8,128)(2,1)} %chain.1), calls=%async_computation.1 | async-start | bytes 524288 | tf_op jit(solution)/shard_map/all_to_all | solution.py:308
  39.6 0.0 copy-start
  39.6 8.7 %inside1.1 = (f32[2048,256]{1,0:T(8,128)}, f32[2048,256]{1,0:T(8,128)}) custom-call(s32[1]{0:T(128)} %bitcast.where_ref, bf16[2048,512]{1,0:T(8,128)(2,1)} %q_ref.5, bf16[2048,512]{1,0:T(8,128)(2,1)} %k_ref.5, bf16[2048,512]{1,0:T(8,128)(2,1)} %v_ref.5, bf16[2048,512]{1,0:T(8,128)(2,1)} %g_ref.5, f32[8,2048]{1,0:T(8,128)} %ld_ref.7), custom_call_target="tpu_custom_call" | custom-call | flops 2147483648 | bytes 8388608 | tf_op jit(solution)/shard_map/inside1/pallas_call | solution.py:170
  48.3 1.0 all-to-all-done.1
  49.4 0.0 copy-done
  49.4 19.5 %finish.1 = (bf16[2048,512]{1,0:T(8,128)(2,1)}, bf16[2048,512]{1,0:T(8,128)(2,1)}, bf16[32,512,128]{2,1,0:T(8,128)(2,1)S(1)}) custom-call(s32[1]{0:T(128)} %bitcast.where_ref, bf16[2,256,256]{2,1,0:T(8,128)(2,1)S(1)} %bitcast.2, f32[4,2,256,256]{3,2,1,0:T(8,128)} %get-tuple-element.21.state_ref, bf16[2048,512]{1,0:T(8,128)(2,1)} %k_ref.5, ...), custom_call_target="tpu_custom_call" | custom-call | flops 9663676416 | bytes 16777216 | tf_op jit(solution)/shard_map/finish/pallas_call | solution.py:242
  68.9 59.0 %all_to_all.15.parts_ref = bf16[32,512,128]{2,1,0:T(8,128)(2,1)S(1)} all-to-all(bf16[32,512,128]{2,1,0:T(8,128)(2,1)S(1)} %get-tuple-element.28), channel_id=1, replica_groups=mesh['z'=4,'x'=4,'y'=2,'lo'=2,'core'=2] {'z','x','y'}, dimensions={0} | all-to-all | bytes 8388608 | tf_op jit(solution)/shard_map/all_to_all | solution.py:313
  127.9 1.4 %gathered.1 = bf16[64,2,512]{2,1,0:T(2,128)(2,1)} custom-call(bf16[32,512,128]{2,1,0:T(8,128)(2,1)S(1)} %all_to_all.15.parts_ref), custom_call_target="tpu_custom_call" | custom-call | flops 2097152 | bytes 4194304 | tf_op jit(solution)/shard_map/gathered/pallas_call | solution.py:289
Async XLA Ops:
  7.9 22.8 %all-to-all-start = ((bf16[32,16,384]{2,1,0:T(8,128)(2,1)}), bf16[32,16,384]{2,1,0:T(8,128)(2,1)S(1)}, u32[]{:S(2)}, u32[]{:S(2)}) async-start(bf16[32,16,384]{2,1,0:T(8,128)(2,1)} %get-tuple-element.16), calls=%async_computation | async-start | bytes 786432 | tf_op jit(solution)/shard_map/all_to_all | solution.py:305
  30.8 0.7 copy-start.1
  33.3 16.1 %all-to-all-start.1 = ((bf16[32,16,256]{2,1,0:T(8,128)(2,1)}), bf16[32,16,256]{2,1,0:T(8,128)(2,1)S(1)}, u32[]{:S(2)}, u32[]{:S(2)}) async-start(bf16[32,16,256]{2,1,0:T(8,128)(2,1)} %chain.1), calls=%async_computation.1 | async-start | bytes 524288 | tf_op jit(solution)/shard_map/all_to_all | solution.py:308
  39.6 9.8 %copy-start = (f32[8,2048]{1,0:T(8,128)S(1)}, f32[8,2048]{1,0:T(8,128)}, u32[]{:S(2)}) copy-start(f32[8,2048]{1,0:T(8,128)} %ld_ref.7) | copy-start | bytes 196612
where the time goes:
time: 132 us; the launch traced here: 129 us
  blocking collectives  59 us (45%)
  Pallas kernels  47.3 us (36%)
  starting transfers between devices  17.6 us (13%)
  waiting for transfers between devices  4 us (3%)
    all_to_all x1, blocking collectives, shards(): parts = lax.all_to_all(parts, SEQ, 0, 0, tiled=True)  59 us
    pallas_call x1, Pallas kernels, finish(): pl.pallas_call(functools.partial(finish_kernel, heads, blocks), grid_spec...  19.5 us
    pallas_call x2, Pallas kernels, inside(): pl.pallas_call(functools.partial(inside_kernel, heads, head), grid_spec=p...  17.2 us
    all_to_all x1, starting transfers between devices, shards(): arrived = lax.all_to_all(message, SEQ, 0, 0, tiled=True)  11.3 us
    pallas_call x1, Pallas kernels, block_states(): pl.pallas_call(functools.partial(states_kernel, heads), grid_spec=pltpu.P...  7.31 us
    all_to_all x1, starting transfers between devices, shards(): carried = lax.all_to_all(chain(arrived), SEQ, 0, 0, tiled=True)  6.28 us
    all_to_all x1, waiting for transfers between devices, shards(): arrived = lax.all_to_all(message, SEQ, 0, 0, tiled=True)  2.96 us
  transfers between devices with their start and end apart: 2, of which 2 were waited for; matrix products, arithmetic and copies ran while one was open for 0% of the time, Pallas kernels for 13%

commit v1 on v0

--- a/solution.py
+++ b/solution.py
@@ -1,4 +1,5 @@
 import functools
+import itertools
 
 import jax
 import jax.numpy as jnp
@@ -19,9 +20,9 @@
 
 
 def cumulate(rows):
-    lane = lax.broadcasted_iota(jnp.int32, rows.shape, 1)
+    lane = lax.rem(lax.broadcasted_iota(jnp.int32, rows.shape, 1), BLOCK)
     step = 1
-    while step < rows.shape[1]:
+    while step < BLOCK:
         rows = rows + jnp.where(lane >= step, pltpu.roll(rows, step, 1), 0.0)
         step *= 2
     return rows
@@ -58,13 +59,21 @@
 
     cum = cumulate(own_rows(ld_ref[...], where_ref[0] * heads, heads))
     decay = (SCALE * jnp.exp(cum)).T
+    before = passed[:, 0:1]
+    sums = [total[h] for h in range(heads)]
+    for c in range(state_ref.shape[0]):
+        rows = slice(c * BLOCK, (c + 1) * BLOCK)
+        kept = jnp.exp(before)
+        for h in range(heads):
+            cols = slice(h * DH, (h + 1) * DH)
+            weighted = (q_ref[rows, cols].astype(F32) * decay[rows, h : h + 1]).astype(BF16)
+            state = dot_tt(weighted, g_ref[rows, cols])
+            state_ref[c, h] = state
+            sums[h] = sums[h] + kept[h : h + 1, :] * state
+        before = before + cum[:, (c + 1) * BLOCK - 1 : (c + 1) * BLOCK]
     for h in range(heads):
-        cols = slice(h * DH, (h + 1) * DH)
-        weighted = (q_ref[:, cols].astype(F32) * decay[:, h : h + 1]).astype(BF16)
-        state = dot_tt(weighted, g_ref[:, cols])
-        state_ref[0, h] = state
-        total[h] = total[h] + jnp.exp(passed[h : h + 1, 0:1]) * state
-    passed[...] = passed[...] + cum[:, BLOCK - 1 : BLOCK]
+        total[h] = sums[h]
+    passed[...] = jnp.broadcast_to(before, passed.shape)
 
     @pl.when(block == pl.num_programs(0) - 1)
     def _():
@@ -88,18 +97,19 @@
     heads = width // DH
     blocks = rows // BLOCK
     piece = heads * DH // devices
+    per = 2
     return pl.pallas_call(
         functools.partial(states_kernel, heads),
         grid_spec=pltpu.PrefetchScalarGridSpec(
             num_scalar_prefetch=1,
-            grid=(blocks,),
+            grid=(blocks // per,),
             in_specs=[
-                pl.BlockSpec((BLOCK, width), lambda i, s: (i, 0)),
-                pl.BlockSpec((BLOCK, width), lambda i, s: (i, 0)),
-                pl.BlockSpec((log_decay.shape[0], BLOCK), lambda i, s: (0, i)),
+                pl.BlockSpec((per * BLOCK, width), lambda i, s: (i, 0)),
+                pl.BlockSpec((per * BLOCK, width), lambda i, s: (i, 0)),
+                pl.BlockSpec((log_decay.shape[0], per * BLOCK), lambda i, s: (0, i)),
             ],
             out_specs=[
-                pl.BlockSpec((1, heads, DH, DH), lambda i, s: (i, 0, 0, 0)),
+                pl.BlockSpec((per, heads, DH, DH), lambda i, s: (i, 0, 0, 0)),
                 pl.BlockSpec((devices, piece, DH + 128), lambda i, s: (0, 0, 0)),
             ],
             scratch_shapes=[pltpu.VMEM((heads, DH, DH), F32), pltpu.VMEM((log_decay.shape[0], 128), F32)],
@@ -132,6 +142,7 @@
         chain_kernel,
         out_shape=jax.ShapeDtypeStruct((devices, piece, DH), BF16),
         cost_estimate=pl.CostEstimate(flops=4 * devices * piece * DH, bytes_accessed=4 * message.size, transcendentals=0),
+        compiler_params=pltpu.CompilerParams(vmem_limit_bytes=8 << 20),
         name="chain",
     )(message)
 
@@ -159,8 +170,8 @@
             to_key, to_value = (dot_tt(grad_scores, q), dot_tt(key_scores, g))
             key_part = to_key if key_part is None else key_part + to_key
             value_part = to_value if value_part is None else value_part + to_value
-        ik_ref[sources, :] = key_part
-        iv_ref[sources, :] = value_part
+        ik_ref[sources, :] = key_part.astype(BF16)
+        iv_ref[sources, :] = value_part.astype(BF16)
 
 
 def inside(place, head, queries, keys, values, out_grad, log_decay):
@@ -175,9 +186,9 @@
             in_specs=[tokens] * 4 + [pl.BlockSpec((log_decay.shape[0], BLOCK), lambda i, s: (0, i))],
             out_specs=[pl.BlockSpec((BLOCK, DH), lambda i, s: (i, 0))] * 2,
         ),
-        out_shape=[jax.ShapeDtypeStruct((rows, DH), F32)] * 2,
+        out_shape=[jax.ShapeDtypeStruct((rows, DH), BF16)] * 2,
         cost_estimate=pl.CostEstimate(
-            flops=8 * rows * DH * BLOCK, bytes_accessed=16 * rows * DH, transcendentals=rows * BLOCK
+            flops=8 * rows * DH * BLOCK, bytes_accessed=12 * rows * DH, transcendentals=rows * BLOCK
         ),
         name=f"inside{head}",
     )(place, queries, keys, values, out_grad, log_decay)
@@ -203,8 +214,8 @@
             cols = slice(h * DH, (h + 1) * DH)
             low = carry[h].astype(BF16)
             over = decayed[:, h : h + 1]
-            key_grad = (inner[2 * h][...] + over * dot_nt(v_ref[:, cols], low)).astype(BF16)
-            value_grad = (inner[2 * h + 1][...] + over * dot_nn(k_ref[:, cols], low)).astype(BF16)
+            key_grad = (inner[2 * h][...].astype(F32) + over * dot_nt(v_ref[:, cols], low)).astype(BF16)
+            value_grad = (inner[2 * h + 1][...].astype(F32) + over * dot_nn(k_ref[:, cols], low)).astype(BF16)
             kg_ref[:, cols] = key_grad
             vg_ref[:, cols] = value_grad
             grads[rows, cols] = key_grad
@@ -213,15 +224,16 @@
 
     @pl.when(step >= blocks)
     def _():
-        devices, share, lanes = out_ref.shape
-        strips = 2 * width // lanes
-        share = share // strips
+        outer = step - blocks
+        share = out_ref.shape[2] // 2
         for part in range(2):
             sums = dot_tt(x_ref[...], grads[:, part * width : (part + 1) * width]).astype(BF16)
-            for d in range(devices):
-                for c in range(width // lanes):
-                    at = (part * (width // lanes) + c) * share
-                    out_ref[d, at : at + share, :] = sums[d * share : (d + 1) * share, c * lanes : (c + 1) * lanes]
+            for inner_axis in range(4):
+                piece = jnp.where(lax.rem(where_ref[0], 2) == 0, outer, inner_axis)
+                slot = jnp.where(lax.rem(where_ref[0], 2) == 0, inner_axis, outer)
+                for y in range(2):
+                    at = (2 * inner_axis + y) * share
+                    out_ref[piece, 2 * slot + y, part * share : (part + 1) * share, :] = sums[at : at + share, :]
 
 
 def finish(place, carried, states, keys, values, log_decay, inner, inputs, devices):
@@ -256,12 +268,12 @@
             out_specs=[
                 tokens,
                 tokens,
-                pl.BlockSpec((devices // steps, 2 * share * width // 128, 128), lambda i, s: (later(i), 0, 0)),
+                pl.BlockSpec((4, devices // 4, 2 * share, width), lambda i, s: (0, 0, 0, 0)),
             ],
             scratch_shapes=[pltpu.VMEM((heads, DH, DH), F32), pltpu.VMEM((rows, 2 * width), BF16)],
         ),
         out_shape=[jax.ShapeDtypeStruct((rows, width), BF16)] * 2
-        + [pltpu.VMEM((devices, 2 * share * width // 128, 128), BF16)],
+        + [pltpu.VMEM((4, devices // 4, 2 * share, width), BF16)],
         cost_estimate=pl.CostEstimate(
             flops=4 * rows * width * (DH + wide), bytes_accessed=16 * rows * width, transcendentals=rows * heads
         ),
@@ -270,30 +282,57 @@
     )(place, carried, states, keys, values, log_decay, *inner, inputs)
 
 
-def gather_kernel(parts_ref, out_ref):
-    devices, rows, lanes = parts_ref.shape
-    share, _, width = out_ref.shape
-    strips = width // lanes
-    step = 32
-    for start in range(0, rows, step):
-        total = parts_ref[0, start : start + step, :].astype(F32)
-        for d in range(1, devices):
-            total = total + parts_ref[d, start : start + step, :].astype(F32)
-        part, strip = divmod(start // share, strips)
+def near_kernel(parts_ref, out_ref):
+    rows = 32
+    for slot in range(out_ref.shape[0]):
+        for at in range(0, out_ref.shape[1], rows):
+            total = parts_ref[0, slot, at : at + rows, :].astype(F32)
+            for p in range(1, parts_ref.shape[0]):
+                total = total + parts_ref[p, slot, at : at + rows, :].astype(F32)
+            out_ref[slot, at : at + rows, :] = total.astype(BF16)
+
+
+def far_kernel(parts_ref, out_ref):
+    rows = 16
+    share = out_ref.shape[0]
+    for start in range(0, parts_ref.shape[1], rows):
+        total = parts_ref[0, start : start + rows, :].astype(F32)
+        for p in range(1, parts_ref.shape[0]):
+            total = total + parts_ref[p, start : start + rows, :].astype(F32)
         at = start % share
-        out_ref[at : at + step, part, strip * lanes : (strip + 1) * lanes] = total.astype(BF16)
-
-
-def gathered(parts, width):
-    rows = parts.shape[1] * parts.shape[2] // width
-    return pl.pallas_call(
-        gather_kernel,
+        out_ref[at : at + rows, start // share, :] = total.astype(BF16)
+
+
+def summed(body, parts, shape, name):
+    return pl.pallas_call(
+        body,
         in_specs=[pl.BlockSpec(memory_space=pltpu.VMEM)],
-        out_shape=jax.ShapeDtypeStruct((rows // 2, 2, width), BF16),
+        out_shape=shape,
         cost_estimate=pl.CostEstimate(flops=parts.size, bytes_accessed=2 * parts.size, transcendentals=0),
         compiler_params=pltpu.CompilerParams(vmem_limit_bytes=12 << 20),
-        name="gathered",
+        name=name,
     )(parts)
+
+
+def groups_of(*axes_of_core):
+    sizes = dict(zip(EVERY, (4, 4, 2, 2, 2)))
+    out = []
+    for core, axes in enumerate(axes_of_core):
+        rest = [axis for axis in SEQ + ("lo",) if axis not in axes]
+        for fixed in itertools.product(*(range(sizes[axis]) for axis in rest)):
+            group = []
+            for varied in itertools.product(*(range(sizes[axis]) for axis in axes)):
+                spot = dict(zip(rest, fixed)) | dict(zip(axes, varied)) | {"core": core}
+                index = 0
+                for axis in EVERY:
+                    index = index * sizes[axis] + spot[axis]
+                group.append(index)
+            out.append(group)
+    return out
+
+
+def exchanged(pieces, *axes_of_core):
+    return lax.all_to_all(pieces, EVERY, 0, 0, axis_index_groups=groups_of(*axes_of_core), tiled=True)
 
 
 def shards(queries, keys, values, out_grad, log_decay, inputs):
@@ -310,8 +349,11 @@
     key_grad, value_grad, parts = finish(
         place, carried.reshape(-1, DH, DH), states, keys, values, log_decay, inner, inputs, devices
     )
-    parts = lax.all_to_all(parts, SEQ, 0, 0, tiled=True)
-    return (key_grad, value_grad, gathered(parts, width))
+    near = exchanged(parts, ("z",), ("x",))
+    near = summed(near_kernel, near, pltpu.VMEM(parts.shape[1:], BF16), "near")
+    far = exchanged(near, ("x", "y"), ("z", "y"))
+    out = jax.ShapeDtypeStruct((parts.shape[2] // 2, 2, width), BF16)
+    return (key_grad, value_grad, summed(far_kernel, far, out, "far"))
 
 
 def solution(mesh):

time: 132 us -> 119 us (0.902); the launches traced: 129 us -> 119 us
  blocking collectives: 59 us -> 52.8 us
  Pallas kernels: 47.3 us -> 43.3 us
    all_to_all x1 -> x2, blocking collectives: 59 us -> 52.8 us  [exchanged(): lax.all_to_all(pieces, EVERY, 0, 0, axis_index_groups=groups_of(*axes_of_...]
    pallas_call x1, Pallas kernels: 7.31 us -> 5.94 us  [block_states(): pl.pallas_call(functools.partial(states_kernel, heads), grid_spec=pltpu.P...]
  transfers between devices with their start and end apart: 2 -> 2, of which waited for: 2 -> 2; matrix products, arithmetic and copies ran while one was open for 0% -> 0% of each run, Pallas kernels for 13% -> 14%
where the time goes in v1:
time: 119 us
  blocking collectives  52.8 us (44%)
  Pallas kernels  43.3 us (36%)
  starting transfers between devices  17.4 us (15%)
  waiting for transfers between devices  4.51 us (4%)
    all_to_all x2, blocking collectives, exchanged(): lax.all_to_all(pieces, EVERY, 0, 0, axis_index_groups=groups_of(*axes_of_...  52.8 us
    pallas_call x1, Pallas kernels, finish(): pl.pallas_call(functools.partial(finish_kernel, heads, blocks), grid_spec...  18.5 us
    pallas_call x2, Pallas kernels, inside(): pl.pallas_call(functools.partial(inside_kernel, heads, head), grid_spec=p...  16.7 us
    all_to_all x1, starting transfers between devices, shards(): arrived = lax.all_to_all(message, SEQ, 0, 0, tiled=True)  11.3 us
    all_to_all x1, starting transfers between devices, shards(): carried = lax.all_to_all(chain(arrived), SEQ, 0, 0, tiled=True)  6.07 us
    pallas_call x1, Pallas kernels, block_states(): pl.pallas_call(functools.partial(states_kernel, heads), grid_spec=pltpu.P...  5.94 us
    all_to_all x1, waiting for transfers between devices, shards(): arrived = lax.all_to_all(message, SEQ, 0, 0, tiled=True)  3.16 us
  transfers between devices with their start and end apart: 2, of which 2 were waited for; matrix products, arithmetic and copies ran while one was open for 0% of the time, Pallas kernels for 14%

profile of v1, /device:TPU:1, one launch (start us, length us, event | category | flops | bytes accessed | tf_op | source)
XLA Modules:
  0.0 118.7 jit_solution(18108622132203253494)
XLA Ops:
  0.6 5.9 %states.1 = (f32[4,2,256,256]{3,2,1,0:T(8,128)}, bf16[32,16,384]{2,1,0:T(8,128)(2,1)}) custom-call(s32[1]{0:T(128)} %bitcast.where_ref, bf16[2048,512]{1,0:T(8,128)(2,1)} %q_ref.5, bf16[2048,512]{1,0:T(8,128)(2,1)} %g_ref.5, f32[8,2048]{1,0:T(8,128)} %ld_ref.7), custom_call_target="tpu_custom_call" | custom-call | flops 536870912 | bytes 6291456 | tf_op jit(solution)/shard_map/states/pallas_call | solution.py:101
  6.6 11.3 %all-to-all-start = ((bf16[32,16,384]{2,1,0:T(8,128)(2,1)}), bf16[32,16,384]{2,1,0:T(8,128)(2,1)S(1)}, u32[]{:S(2)}, u32[]{:S(2)}) async-start(bf16[32,16,384]{2,1,0:T(8,128)(2,1)} %get-tuple-element.16), calls=%async_computation | async-start | bytes 786432 | tf_op jit(solution)/shard_map/all_to_all | solution.py:344
  17.9 8.3 %inside0.1 = (bf16[2048,256]{1,0:T(8,128)(2,1)}, bf16[2048,256]{1,0:T(8,128)(2,1)}) custom-call(s32[1]{0:T(128)} %bitcast.where_ref, bf16[2048,512]{1,0:T(8,128)(2,1)} %q_ref.5, bf16[2048,512]{1,0:T(8,128)(2,1)} %k_ref.5, bf16[2048,512]{1,0:T(8,128)(2,1)} %v_ref.5, bf16[2048,512]{1,0:T(8,128)(2,1)} %g_ref.5, f32[8,2048]{1,0:T(8,128)} %ld_ref.7), custom_call_target="tpu_custom_call" | custom-call | flops 2147483648 | bytes 6291456 | tf_op jit(solution)/shard_map/inside0/pallas_call | solution.py:181
  26.2 3.2 %all-to-all-done.message_ref = bf16[32,16,384]{2,1,0:T(8,128)(2,1)S(1)} async-done(((bf16[32,16,384]{2,1,0:T(8,128)(2,1)}), bf16[32,16,384]{2,1,0:T(8,128)(2,1)S(1)}, u32[]{:S(2)}, u32[]{:S(2)}) %all-to-all-start) | async-done | bytes 393248 | tf_op jit(solution)/shard_map/all_to_all | solution.py:344
  29.4 0.8 chain.1
  30.2 6.1 %all-to-all-start.1 = ((bf16[32,16,256]{2,1,0:T(8,128)(2,1)}), bf16[32,16,256]{2,1,0:T(8,128)(2,1)S(1)}, u32[]{:S(2)}, u32[]{:S(2)}) async-start(bf16[32,16,256]{2,1,0:T(8,128)(2,1)} %chain.1), calls=%async_computation.1 | async-start | bytes 524288 | tf_op jit(solution)/shard_map/all_to_all | solution.py:347
  36.3 0.0 copy-start
  36.3 0.0 copy-start.1
  36.3 8.4 %inside1.1 = (bf16[2048,256]{1,0:T(8,128)(2,1)}, bf16[2048,256]{1,0:T(8,128)(2,1)}) custom-call(s32[1]{0:T(128)} %bitcast.where_ref, bf16[2048,512]{1,0:T(8,128)(2,1)} %q_ref.5, bf16[2048,512]{1,0:T(8,128)(2,1)} %k_ref.5, bf16[2048,512]{1,0:T(8,128)(2,1)} %v_ref.5, bf16[2048,512]{1,0:T(8,128)(2,1)} %g_ref.5, f32[8,2048]{1,0:T(8,128)} %ld_ref.7), custom_call_target="tpu_custom_call" | custom-call | flops 2147483648 | bytes 6291456 | tf_op jit(solution)/shard_map/inside1/pallas_call | solution.py:181
  44.7 1.4 %all-to-all-done.1 = bf16[32,16,256]{2,1,0:T(8,128)(2,1)S(1)} async-done(((bf16[32,16,256]{2,1,0:T(8,128)(2,1)}), bf16[32,16,256]{2,1,0:T(8,128)(2,1)S(1)}, u32[]{:S(2)}, u32[]{:S(2)}) %all-to-all-start.1) | async-done | bytes 262176 | tf_op jit(solution)/shard_map/all_to_all | solution.py:347
  46.1 0.0 copy-done
  46.1 0.0 copy-done.1
  46.1 18.5 %finish.1 = (bf16[2048,512]{1,0:T(8,128)(2,1)}, bf16[2048,512]{1,0:T(8,128)(2,1)}, bf16[4,8,128,512]{3,2,1,0:T(8,128)(2,1)S(1)}) custom-call(s32[1]{0:T(128)} %bitcast.where_ref, bf16[2,256,256]{2,1,0:T(8,128)(2,1)S(1)} %bitcast.2, f32[4,2,256,256]{3,2,1,0:T(8,128)} %get-tuple-element.21.state_ref, bf16[2048,512]{1,0:T(8,128)(2,1)} %k_ref.5, ...), custom_call_target="tpu_custom_call" | custom-call | flops 9663676416 | bytes 16777216 | tf_op jit(solution)/shard_map/finish/pallas_call | solution.py:254
  64.5 29.4 %all_to_all.20.parts_ref = bf16[4,8,128,512]{3,2,1,0:T(8,128)(2,1)S(1)} all-to-all(bf16[4,8,128,512]{3,2,1,0:T(8,128)(2,1)S(1)} %get-tuple-element.28), channel_id=1, replica_groups={{0,32,64,96},{2,34,66,98},{4,36,68,100},{6,38,70,102},{8,40,72,104},{10..., dimensions={0} | all-to-all | bytes 8388608 | tf_op jit(solution)/shard_map/all_to_all | solution.py:335
  94.0 0.5 near.1
  94.5 23.3 %all_to_all.21.parts_ref = bf16[8,128,512]{2,1,0:T(8,128)(2,1)S(1)} all-to-all(bf16[8,128,512]{2,1,0:T(8,128)(2,1)S(1)} %near.1), channel_id=1, replica_groups={{0,4,8,12,16,20,24,28},{2,6,10,14,18,22,26,30},{32,36,40,44,48,52,56,60..., dimensions={0} | all-to-all | bytes 2097152 | tf_op jit(solution)/shard_map/all_to_all | solution.py:335
  117.8 0.9 far.1
Async XLA Ops:
  6.6 22.8 %all-to-all-start = ((bf16[32,16,384]{2,1,0:T(8,128)(2,1)}), bf16[32,16,384]{2,1,0:T(8,128)(2,1)S(1)}, u32[]{:S(2)}, u32[]{:S(2)}) async-start(bf16[32,16,384]{2,1,0:T(8,128)(2,1)} %get-tuple-element.16), calls=%async_computation | async-start | bytes 786432 | tf_op jit(solution)/shard_map/all_to_all | solution.py:344
  30.2 15.9 %all-to-all-start.1 = ((bf16[32,16,256]{2,1,0:T(8,128)(2,1)}), bf16[32,16,256]{2,1,0:T(8,128)(2,1)S(1)}, u32[]{:S(2)}, u32[]{:S(2)}) async-start(bf16[32,16,256]{2,1,0:T(8,128)(2,1)} %chain.1), calls=%async_computation.1 | async-start | bytes 524288 | tf_op jit(solution)/shard_map/all_to_all | solution.py:347
  36.3 9.8 %copy-start = (f32[8,2048]{1,0:T(8,128)S(1)}, f32[8,2048]{1,0:T(8,128)}, u32[]{:S(2)}) copy-start(f32[8,2048]{1,0:T(8,128)} %ld_ref.7) | copy-start | bytes 196612
  36.3 9.8 %copy-start.1 = (bf16[2048,256]{1,0:T(8,128)(2,1)S(1)}, bf16[2048,256]{1,0:T(8,128)(2,1)}, u32[]{:S(2)}) copy-start(bf16[2048,256]{1,0:T(8,128)(2,1)} %get-tuple-element.22.refs_0_) | copy-start | bytes 3145732

commit v2 on v1

--- a/solution.py
+++ b/solution.py
@@ -116,7 +116,7 @@
         ),
         out_shape=[
             jax.ShapeDtypeStruct((blocks, heads, DH, DH), F32),
-            jax.ShapeDtypeStruct((devices, piece, DH + 128), BF16),
+            pltpu.VMEM((devices, piece, DH + 128), BF16),
         ],
         cost_estimate=pl.CostEstimate(
             flops=2 * rows * width * DH, bytes_accessed=4 * rows * width + 4 * blocks * width * DH, transcendentals=rows
@@ -140,7 +140,7 @@
     devices, piece, _ = message.shape
     return pl.pallas_call(
         chain_kernel,
-        out_shape=jax.ShapeDtypeStruct((devices, piece, DH), BF16),
+        out_shape=pltpu.VMEM((devices, piece, DH), BF16),
         cost_estimate=pl.CostEstimate(flops=4 * devices * piece * DH, bytes_accessed=4 * message.size, transcendentals=0),
         compiler_params=pltpu.CompilerParams(vmem_limit_bytes=8 << 20),
         name="chain",
@@ -154,37 +154,39 @@
     row = lax.broadcasted_iota(jnp.int32, (half, half), 0)
     column = lax.broadcasted_iota(jnp.int32, (half, half), 1)
     seen = row >= column
-    for j in range(2):
-        sources = slice(j * half, (j + 1) * half)
-        k, v = (k_ref[sources, :], v_ref[sources, :])
-        key_part = value_part = None
-        for i in range(j, 2):
-            targets = slice(i * half, (i + 1) * half)
-            q, g = (q_ref[targets, :], g_ref[targets, :])
-            spread = columns[targets, head : head + 1] - cum[head : head + 1, sources]
-            weights = SCALE * jnp.exp(jnp.minimum(spread, 0.0))
-            if i == j:
-                weights = jnp.where(seen, weights, 0.0)
-            key_scores = (dot_nt(q, k) * weights).astype(BF16)
-            grad_scores = (dot_nt(g, v) * weights).astype(BF16)
-            to_key, to_value = (dot_tt(grad_scores, q), dot_tt(key_scores, g))
-            key_part = to_key if key_part is None else key_part + to_key
-            value_part = to_value if value_part is None else value_part + to_value
-        ik_ref[sources, :] = key_part.astype(BF16)
-        iv_ref[sources, :] = value_part.astype(BF16)
+    for c in range(q_ref.shape[0] // BLOCK):
+        for j in range(2):
+            sources = slice(c * BLOCK + j * half, c * BLOCK + (j + 1) * half)
+            k, v = (k_ref[sources, :], v_ref[sources, :])
+            key_part = value_part = None
+            for i in range(j, 2):
+                targets = slice(c * BLOCK + i * half, c * BLOCK + (i + 1) * half)
+                q, g = (q_ref[targets, :], g_ref[targets, :])
+                spread = columns[targets, head : head + 1] - cum[head : head + 1, sources]
+                weights = SCALE * jnp.exp(jnp.minimum(spread, 0.0))
+                if i == j:
+                    weights = jnp.where(seen, weights, 0.0)
+                key_scores = (dot_nt(q, k) * weights).astype(BF16)
+                grad_scores = (dot_nt(g, v) * weights).astype(BF16)
+                to_key, to_value = (dot_tt(grad_scores, q), dot_tt(key_scores, g))
+                key_part = to_key if key_part is None else key_part + to_key
+                value_part = to_value if value_part is None else value_part + to_value
+            ik_ref[sources, :] = key_part.astype(BF16)
+            iv_ref[sources, :] = value_part.astype(BF16)
 
 
 def inside(place, head, queries, keys, values, out_grad, log_decay):
     rows, width = queries.shape
     heads = width // DH
-    tokens = pl.BlockSpec((BLOCK, DH), lambda i, s: (i, head))
+    per = 2 * BLOCK
+    tokens = pl.BlockSpec((per, DH), lambda i, s: (i, head))
     return pl.pallas_call(
         functools.partial(inside_kernel, heads, head),
         grid_spec=pltpu.PrefetchScalarGridSpec(
             num_scalar_prefetch=1,
-            grid=(rows // BLOCK,),
-            in_specs=[tokens] * 4 + [pl.BlockSpec((log_decay.shape[0], BLOCK), lambda i, s: (0, i))],
-            out_specs=[pl.BlockSpec((BLOCK, DH), lambda i, s: (i, 0))] * 2,
+            grid=(rows // per,),
+            in_specs=[tokens] * 4 + [pl.BlockSpec((log_decay.shape[0], per), lambda i, s: (0, i))],
+            out_specs=[pl.BlockSpec((per, DH), lambda i, s: (i, 0))] * 2,
         ),
         out_shape=[jax.ShapeDtypeStruct((rows, DH), BF16)] * 2,
         cost_estimate=pl.CostEstimate(
@@ -194,81 +196,93 @@
     )(place, queries, keys, values, out_grad, log_decay)
 
 
-def finish_kernel(heads, blocks, where_ref, c_ref, state_ref, k_ref, v_ref, ld_ref, *refs):
+def finish_kernel(heads, steps, where_ref, c_ref, state_ref, k_ref, v_ref, ld_ref, *refs):
     inner = refs[: 2 * heads]
-    x_ref, kg_ref, vg_ref, out_ref, carry, grads = refs[2 * heads :]
+    *x_refs, kg_ref, vg_ref, out_ref, carry, grads = refs[2 * heads :]
     step = pl.program_id(0)
     width = heads * DH
+    per = state_ref.shape[0]
 
     @pl.when(step == 0)
     def _():
         carry[...] = c_ref[...].astype(F32)
 
-    @pl.when(step < blocks)
+    @pl.when(step < steps)
     def _():
         cum = cumulate(own_rows(ld_ref[...], where_ref[0] * heads, heads))
-        last = cum[:, BLOCK - 1 : BLOCK]
-        decayed = jnp.exp(last - cum).T
-        rows = pl.ds(pl.multiple_of((blocks - 1 - step) * BLOCK, BLOCK), BLOCK)
+        lasts = [cum[:, (c + 1) * BLOCK - 1 : (c + 1) * BLOCK] for c in range(per)]
+        base = jnp.concatenate([jnp.broadcast_to(last, (cum.shape[0], BLOCK)) for last in lasts], axis=1)
+        decayed = jnp.exp(base - cum).T
+        carries = [carry[h] for h in range(heads)]
+        for c in reversed(range(per)):
+            here = slice(c * BLOCK, (c + 1) * BLOCK)
+            there = pl.ds(pl.multiple_of(((steps - 1 - step) * per + c) * BLOCK, BLOCK), BLOCK)
+            kept = jnp.exp(lasts[c])
+            for h in range(heads):
+                cols = slice(h * DH, (h + 1) * DH)
+                low = carries[h].astype(BF16)
+                over = decayed[here, h : h + 1]
+                key_grad = (inner[2 * h][here, :].astype(F32) + over * dot_nt(v_ref[here, cols], low)).astype(BF16)
+                value_grad = (inner[2 * h + 1][here, :].astype(F32) + over * dot_nn(k_ref[here, cols], low)).astype(BF16)
+                kg_ref[here, cols] = key_grad
+                vg_ref[here, cols] = value_grad
+                grads[there, cols] = key_grad
+                grads[there, width + h * DH : width + (h + 1) * DH] = value_grad
+                carries[h] = kept[h : h + 1, :] * carries[h] + state_ref[c, h]
         for h in range(heads):
-            cols = slice(h * DH, (h + 1) * DH)
-            low = carry[h].astype(BF16)
-            over = decayed[:, h : h + 1]
-            key_grad = (inner[2 * h][...].astype(F32) + over * dot_nt(v_ref[:, cols], low)).astype(BF16)
-            value_grad = (inner[2 * h + 1][...].astype(F32) + over * dot_nn(k_ref[:, cols], low)).astype(BF16)
-            kg_ref[:, cols] = key_grad
-            vg_ref[:, cols] = value_grad
-            grads[rows, cols] = key_grad
-            grads[rows, width + h * DH : width + (h + 1) * DH] = value_grad
-            carry[h] = jnp.exp(last[h : h + 1, :]) * carry[h] + state_ref[0, h]
-
-    @pl.when(step >= blocks)
-    def _():
-        outer = step - blocks
-        share = out_ref.shape[2] // 2
+            carry[h] = carries[h]
+
+    @pl.when(step >= steps)
+    def _():
+        slots, share, _ = out_ref.shape[1:]
+        share = share // 2
+        x = jnp.concatenate([ref[...] for ref in x_refs], axis=1)
         for part in range(2):
-            sums = dot_tt(x_ref[...], grads[:, part * width : (part + 1) * width]).astype(BF16)
-            for inner_axis in range(4):
-                piece = jnp.where(lax.rem(where_ref[0], 2) == 0, outer, inner_axis)
-                slot = jnp.where(lax.rem(where_ref[0], 2) == 0, inner_axis, outer)
-                for y in range(2):
-                    at = (2 * inner_axis + y) * share
-                    out_ref[piece, 2 * slot + y, part * share : (part + 1) * share, :] = sums[at : at + share, :]
+            sums = dot_tt(x, grads[:, part * width : (part + 1) * width]).astype(BF16)
+            for d in range(slots):
+                out_ref[0, d, part * share : (part + 1) * share, :] = sums[d * share : (d + 1) * share, :]
 
 
 def finish(place, carried, states, keys, values, log_decay, inner, inputs, devices):
     rows, width = keys.shape
     heads = width // DH
     blocks = rows // BLOCK
-    steps = 4
+    per = 2
+    steps = blocks // per
     wide = inputs.shape[1]
     share = wide // devices
 
     def back(i):
-        return jnp.maximum(blocks - 1 - i, 0)
+        return jnp.maximum(steps - 1 - i, 0)
 
     def later(i):
-        return jnp.maximum(i - blocks, 0)
-
-    tokens = pl.BlockSpec((BLOCK, width), lambda i, s: (back(i), 0))
-    return pl.pallas_call(
-        functools.partial(finish_kernel, heads, blocks),
+        return jnp.maximum(i - steps, 0)
+
+    def columns(k):
+        return pl.BlockSpec(
+            (rows, wide // 16),
+            lambda i, s: (0, jnp.where(lax.rem(s[0], 2) == 0, 4 * later(i) + k, 4 * k + later(i))),
+        )
+
+    tokens = pl.BlockSpec((per * BLOCK, width), lambda i, s: (back(i), 0))
+    return pl.pallas_call(
+        functools.partial(finish_kernel, heads, steps),
         grid_spec=pltpu.PrefetchScalarGridSpec(
             num_scalar_prefetch=1,
-            grid=(blocks + steps,),
+            grid=(steps + 4,),
             in_specs=[
                 pl.BlockSpec((heads, DH, DH), lambda i, s: (0, 0, 0)),
-                pl.BlockSpec((1, heads, DH, DH), lambda i, s: (back(i), 0, 0, 0)),
+                pl.BlockSpec((per, heads, DH, DH), lambda i, s: (back(i), 0, 0, 0)),
                 tokens,
                 tokens,
-                pl.BlockSpec((log_decay.shape[0], BLOCK), lambda i, s: (0, back(i))),
+                pl.BlockSpec((log_decay.shape[0], per * BLOCK), lambda i, s: (0, back(i))),
             ]
-            + [pl.BlockSpec((BLOCK, DH), lambda i, s: (back(i), 0))] * (2 * heads)
-            + [pl.BlockSpec((rows, wide // steps), lambda i, s: (0, later(i)))],
+            + [pl.BlockSpec((per * BLOCK, DH), lambda i, s: (back(i), 0))] * (2 * heads)
+            + [columns(k) for k in range(4)],
             out_specs=[
                 tokens,
                 tokens,
-                pl.BlockSpec((4, devices // 4, 2 * share, width), lambda i, s: (0, 0, 0, 0)),
+                pl.BlockSpec((1, devices // 4, 2 * share, width), lambda i, s: (later(i), 0, 0, 0)),
             ],
             scratch_shapes=[pltpu.VMEM((heads, DH, DH), F32), pltpu.VMEM((rows, 2 * width), BF16)],
         ),
@@ -279,7 +293,7 @@
         ),
         compiler_params=pltpu.CompilerParams(vmem_limit_bytes=48 << 20),
         name="finish",
-    )(place, carried, states, keys, values, log_decay, *inner, inputs)
+    )(place, carried, states, keys, values, log_decay, *inner, inputs, inputs, inputs, inputs)
 
 
 def near_kernel(parts_ref, out_ref):

time: 119 us -> 117 us (0.983)
  Pallas kernels: 43.3 us -> 41.4 us
  transfers between devices with their start and end apart: 2 -> 2, of which waited for: 2 -> 2; matrix products, arithmetic and copies ran while one was open for 0% -> 0% of each run, Pallas kernels for 14% -> 13%
where the time goes in v2:
time: 117 us
  blocking collectives  52.4 us (45%)
  Pallas kernels  41.4 us (35%)
  starting transfers between devices  16.7 us (14%)
  waiting for transfers between devices  5.65 us (5%)
    all_to_all x2, blocking collectives, exchanged(): lax.all_to_all(pieces, EVERY, 0, 0, axis_index_groups=groups_of(*axes_of_...  52.4 us
    pallas_call x1, Pallas kernels, finish(): pl.pallas_call(functools.partial(finish_kernel, heads, steps), grid_spec=...  17.7 us
    pallas_call x2, Pallas kernels, inside(): pl.pallas_call(functools.partial(inside_kernel, heads, head), grid_spec=p...  15.6 us
    all_to_all x1, starting transfers between devices, shards(): arrived = lax.all_to_all(message, SEQ, 0, 0, tiled=True)  11.3 us
    pallas_call x1, Pallas kernels, block_states(): pl.pallas_call(functools.partial(states_kernel, heads), grid_spec=pltpu.P...  5.94 us
    all_to_all x1, starting transfers between devices, shards(): carried = lax.all_to_all(chain(arrived), SEQ, 0, 0, tiled=True)  5.36 us
    all_to_all x1, waiting for transfers between devices, shards(): arrived = lax.all_to_all(message, SEQ, 0, 0, tiled=True)  3.88 us
  transfers between devices with their start and end apart: 2, of which 2 were waited for; matrix products, arithmetic and copies ran while one was open for 0% of the time, Pallas kernels for 13%

profile of v2, /device:TPU:1, one launch (start us, length us, event | category | flops | bytes accessed | tf_op | source)
XLA Modules:
  0.0 116.8 jit_solution(810881924943752984)
XLA Ops:
  0.6 5.9 %states.1 = (f32[4,2,256,256]{3,2,1,0:T(8,128)}, bf16[32,16,384]{2,1,0:T(8,128)(2,1)}) custom-call(s32[1]{0:T(128)} %bitcast.where_ref, bf16[2048,512]{1,0:T(8,128)(2,1)} %q_ref.5, bf16[2048,512]{1,0:T(8,128)(2,1)} %g_ref.5, f32[8,2048]{1,0:T(8,128)} %ld_ref.7), custom_call_target="tpu_custom_call" | custom-call | flops 536870912 | bytes 6291456 | tf_op jit(solution)/shard_map/states/pallas_call | solution.py:101
  6.6 11.3 %all-to-all-start = ((bf16[32,16,384]{2,1,0:T(8,128)(2,1)}), bf16[32,16,384]{2,1,0:T(8,128)(2,1)S(1)}, u32[]{:S(2)}, u32[]{:S(2)}) async-start(bf16[32,16,384]{2,1,0:T(8,128)(2,1)} %get-tuple-element.16), calls=%async_computation | async-start | bytes 786432 | tf_op jit(solution)/shard_map/all_to_all | solution.py:358
  17.9 7.6 %inside0.1 = (bf16[2048,256]{1,0:T(8,128)(2,1)}, bf16[2048,256]{1,0:T(8,128)(2,1)}) custom-call(s32[1]{0:T(128)} %bitcast.where_ref, bf16[2048,512]{1,0:T(8,128)(2,1)} %q_ref.5, bf16[2048,512]{1,0:T(8,128)(2,1)} %k_ref.5, bf16[2048,512]{1,0:T(8,128)(2,1)} %v_ref.5, bf16[2048,512]{1,0:T(8,128)(2,1)} %g_ref.5, f32[8,2048]{1,0:T(8,128)} %ld_ref.7), custom_call_target="tpu_custom_call" | custom-call | flops 2147483648 | bytes 6291456 | tf_op jit(solution)/shard_map/inside0/pallas_call | solution.py:183
  25.5 3.9 %all-to-all-done.message_ref = bf16[32,16,384]{2,1,0:T(8,128)(2,1)S(1)} async-done(((bf16[32,16,384]{2,1,0:T(8,128)(2,1)}), bf16[32,16,384]{2,1,0:T(8,128)(2,1)S(1)}, u32[]{:S(2)}, u32[]{:S(2)}) %all-to-all-start) | async-done | bytes 393248 | tf_op jit(solution)/shard_map/all_to_all | solution.py:358
  29.4 0.8 chain.1
  30.2 5.4 %all-to-all-start.1 = ((bf16[32,16,256]{2,1,0:T(8,128)(2,1)}), bf16[32,16,256]{2,1,0:T(8,128)(2,1)S(1)}, u32[]{:S(2)}, u32[]{:S(2)}) async-start(bf16[32,16,256]{2,1,0:T(8,128)(2,1)} %chain.1), calls=%async_computation.1 | async-start | bytes 524288 | tf_op jit(solution)/shard_map/all_to_all | solution.py:361
  35.6 0.0 copy-start
  35.6 0.0 copy-start.1
  35.6 8.0 %inside1.1 = (bf16[2048,256]{1,0:T(8,128)(2,1)}, bf16[2048,256]{1,0:T(8,128)(2,1)}) custom-call(s32[1]{0:T(128)} %bitcast.where_ref, bf16[2048,512]{1,0:T(8,128)(2,1)} %q_ref.5, bf16[2048,512]{1,0:T(8,128)(2,1)} %k_ref.5, bf16[2048,512]{1,0:T(8,128)(2,1)} %v_ref.5, bf16[2048,512]{1,0:T(8,128)(2,1)} %g_ref.5, f32[8,2048]{1,0:T(8,128)} %ld_ref.7), custom_call_target="tpu_custom_call" | custom-call | flops 2147483648 | bytes 6291456 | tf_op jit(solution)/shard_map/inside1/pallas_call | solution.py:183
  43.6 1.8 %all-to-all-done.1 = bf16[32,16,256]{2,1,0:T(8,128)(2,1)S(1)} async-done(((bf16[32,16,256]{2,1,0:T(8,128)(2,1)}), bf16[32,16,256]{2,1,0:T(8,128)(2,1)S(1)}, u32[]{:S(2)}, u32[]{:S(2)}) %all-to-all-start.1) | async-done | bytes 262176 | tf_op jit(solution)/shard_map/all_to_all | solution.py:361
  45.3 0.0 copy-done
  45.4 0.0 copy-done.1
  45.4 17.7 %finish.1 = (bf16[2048,512]{1,0:T(8,128)(2,1)}, bf16[2048,512]{1,0:T(8,128)(2,1)}, bf16[4,8,128,512]{3,2,1,0:T(8,128)(2,1)S(1)}) custom-call(s32[1]{0:T(128)} %bitcast.where_ref, bf16[2,256,256]{2,1,0:T(8,128)(2,1)S(1)} %bitcast.2, f32[4,2,256,256]{3,2,1,0:T(8,128)} %get-tuple-element.21.state_ref, bf16[2048,512]{1,0:T(8,128)(2,1)} %k_ref.5, ...), custom_call_target="tpu_custom_call" | custom-call | flops 9663676416 | bytes 16777216 | tf_op jit(solution)/shard_map/finish/pallas_call | solution.py:268
  63.1 29.4 %all_to_all.20.parts_ref = bf16[4,8,128,512]{3,2,1,0:T(8,128)(2,1)S(1)} all-to-all(bf16[4,8,128,512]{3,2,1,0:T(8,128)(2,1)S(1)} %get-tuple-element.28), channel_id=1, replica_groups={{0,32,64,96},{2,34,66,98},{4,36,68,100},{6,38,70,102},{8,40,72,104},{10..., dimensions={0} | all-to-all | bytes 8388608 | tf_op jit(solution)/shard_map/all_to_all | solution.py:349
  92.5 0.5 near.1
  93.1 22.9 %all_to_all.21.parts_ref = bf16[8,128,512]{2,1,0:T(8,128)(2,1)S(1)} all-to-all(bf16[8,128,512]{2,1,0:T(8,128)(2,1)S(1)} %near.1), channel_id=1, replica_groups={{0,4,8,12,16,20,24,28},{2,6,10,14,18,22,26,30},{32,36,40,44,48,52,56,60..., dimensions={0} | all-to-all | bytes 2097152 | tf_op jit(solution)/shard_map/all_to_all | solution.py:349
  116.0 0.9 far.1
Async XLA Ops:
  6.6 22.8 %all-to-all-start = ((bf16[32,16,384]{2,1,0:T(8,128)(2,1)}), bf16[32,16,384]{2,1,0:T(8,128)(2,1)S(1)}, u32[]{:S(2)}, u32[]{:S(2)}) async-start(bf16[32,16,384]{2,1,0:T(8,128)(2,1)} %get-tuple-element.16), calls=%async_computation | async-start | bytes 786432 | tf_op jit(solution)/shard_map/all_to_all | solution.py:358
  30.2 15.1 %all-to-all-start.1 = ((bf16[32,16,256]{2,1,0:T(8,128)(2,1)}), bf16[32,16,256]{2,1,0:T(8,128)(2,1)S(1)}, u32[]{:S(2)}, u32[]{:S(2)}) async-start(bf16[32,16,256]{2,1,0:T(8,128)(2,1)} %chain.1), calls=%async_computation.1 | async-start | bytes 524288 | tf_op jit(solution)/shard_map/all_to_all | solution.py:361
  35.6 9.8 %copy-start = (f32[8,2048]{1,0:T(8,128)S(1)}, f32[8,2048]{1,0:T(8,128)}, u32[]{:S(2)}) copy-start(f32[8,2048]{1,0:T(8,128)} %ld_ref.7) | copy-start | bytes 196612
  35.6 9.8 %copy-start.1 = (bf16[2048,256]{1,0:T(8,128)(2,1)S(1)}, bf16[2048,256]{1,0:T(8,128)(2,1)}, u32[]{:S(2)}) copy-start(bf16[2048,256]{1,0:T(8,128)(2,1)} %get-tuple-element.22.refs_0_) | copy-start | bytes 3145732

commit v3 on v2

--- a/solution.py
+++ b/solution.py
@@ -153,7 +153,7 @@
     half = BLOCK // 2
     row = lax.broadcasted_iota(jnp.int32, (half, half), 0)
     column = lax.broadcasted_iota(jnp.int32, (half, half), 1)
-    seen = row >= column
+    seen = column >= row
     for c in range(q_ref.shape[0] // BLOCK):
         for j in range(2):
             sources = slice(c * BLOCK + j * half, c * BLOCK + (j + 1) * half)
@@ -162,13 +162,13 @@
             for i in range(j, 2):
                 targets = slice(c * BLOCK + i * half, c * BLOCK + (i + 1) * half)
                 q, g = (q_ref[targets, :], g_ref[targets, :])
-                spread = columns[targets, head : head + 1] - cum[head : head + 1, sources]
+                spread = cum[head : head + 1, targets] - columns[sources, head : head + 1]
                 weights = SCALE * jnp.exp(jnp.minimum(spread, 0.0))
                 if i == j:
                     weights = jnp.where(seen, weights, 0.0)
-                key_scores = (dot_nt(q, k) * weights).astype(BF16)
-                grad_scores = (dot_nt(g, v) * weights).astype(BF16)
-                to_key, to_value = (dot_tt(grad_scores, q), dot_tt(key_scores, g))
+                key_scores = (dot_nt(k, q) * weights).astype(BF16)
+                grad_scores = (dot_nt(v, g) * weights).astype(BF16)
+                to_key, to_value = (dot_nn(grad_scores, q), dot_nn(key_scores, g))
                 key_part = to_key if key_part is None else key_part + to_key
                 value_part = to_value if value_part is None else value_part + to_value
             ik_ref[sources, :] = key_part.astype(BF16)

time: 117 us -> 115 us (0.983)
  Pallas kernels: 41.4 us -> 39.3 us
  waiting for transfers between devices: 5.65 us -> 7.74 us
    pallas_call x2, Pallas kernels: 15.6 us -> 13.5 us  [inside(): pl.pallas_call(functools.partial(inside_kernel, heads, head), grid_spec=p...]
  transfers between devices with their start and end apart: 2 -> 2, of which waited for: 2 -> 2; matrix products, arithmetic and copies ran while one was open for 0% -> 0% of each run, Pallas kernels for 13% -> 12%
where the time goes in v3:
time: 115 us
  blocking collectives  51.3 us (45%)
  Pallas kernels  39.3 us (34%)
  starting transfers between devices  15.7 us (14%)
  waiting for transfers between devices  7.74 us (7%)
    all_to_all x2, blocking collectives, exchanged(): lax.all_to_all(pieces, EVERY, 0, 0, axis_index_groups=groups_of(*axes_of_...  51.3 us
    pallas_call x1, Pallas kernels, finish(): pl.pallas_call(functools.partial(finish_kernel, heads, steps), grid_spec=...  17.7 us
    pallas_call x2, Pallas kernels, inside(): pl.pallas_call(functools.partial(inside_kernel, heads, head), grid_spec=p...  13.5 us
    all_to_all x1, starting transfers between devices, shards(): arrived = lax.all_to_all(message, SEQ, 0, 0, tiled=True)  11.3 us
    pallas_call x1, Pallas kernels, block_states(): pl.pallas_call(functools.partial(states_kernel, heads), grid_spec=pltpu.P...  5.94 us
    all_to_all x1, waiting for transfers between devices, shards(): arrived = lax.all_to_all(message, SEQ, 0, 0, tiled=True)  4.92 us
    all_to_all x1, starting transfers between devices, shards(): carried = lax.all_to_all(chain(arrived), SEQ, 0, 0, tiled=True)  4.32 us
    all_to_all x1, waiting for transfers between devices, shards(): carried = lax.all_to_all(chain(arrived), SEQ, 0, 0, tiled=True)  2.83 us
  transfers between devices with their start and end apart: 2, of which 2 were waited for; matrix products, arithmetic and copies ran while one was open for 0% of the time, Pallas kernels for 12%

profile of v3, /device:TPU:1, one launch (start us, length us, event | category | flops | bytes accessed | tf_op | source)
XLA Modules:
  0.0 114.8 jit_solution(1362010229462420507)
XLA Ops:
  0.6 5.9 %states.1 = (f32[4,2,256,256]{3,2,1,0:T(8,128)}, bf16[32,16,384]{2,1,0:T(8,128)(2,1)}) custom-call(s32[1]{0:T(128)} %bitcast.where_ref, bf16[2048,512]{1,0:T(8,128)(2,1)} %q_ref.5, bf16[2048,512]{1,0:T(8,128)(2,1)} %g_ref.5, f32[8,2048]{1,0:T(8,128)} %ld_ref.7), custom_call_target="tpu_custom_call" | custom-call | flops 536870912 | bytes 6291456 | tf_op jit(solution)/shard_map/states/pallas_call | solution.py:101
  6.6 11.3 %all-to-all-start = ((bf16[32,16,384]{2,1,0:T(8,128)(2,1)}), bf16[32,16,384]{2,1,0:T(8,128)(2,1)S(1)}, u32[]{:S(2)}, u32[]{:S(2)}) async-start(bf16[32,16,384]{2,1,0:T(8,128)(2,1)} %get-tuple-element.16), calls=%async_computation | async-start | bytes 786432 | tf_op jit(solution)/shard_map/all_to_all | solution.py:358
  17.9 6.6 %inside0.1 = (bf16[2048,256]{1,0:T(8,128)(2,1)}, bf16[2048,256]{1,0:T(8,128)(2,1)}) custom-call(s32[1]{0:T(128)} %bitcast.where_ref, bf16[2048,512]{1,0:T(8,128)(2,1)} %q_ref.5, bf16[2048,512]{1,0:T(8,128)(2,1)} %k_ref.5, bf16[2048,512]{1,0:T(8,128)(2,1)} %v_ref.5, bf16[2048,512]{1,0:T(8,128)(2,1)} %g_ref.5, f32[8,2048]{1,0:T(8,128)} %ld_ref.7), custom_call_target="tpu_custom_call" | custom-call | flops 2147483648 | bytes 6291456 | tf_op jit(solution)/shard_map/inside0/pallas_call | solution.py:183
  24.5 4.9 %all-to-all-done.message_ref = bf16[32,16,384]{2,1,0:T(8,128)(2,1)S(1)} async-done(((bf16[32,16,384]{2,1,0:T(8,128)(2,1)}), bf16[32,16,384]{2,1,0:T(8,128)(2,1)S(1)}, u32[]{:S(2)}, u32[]{:S(2)}) %all-to-all-start) | async-done | bytes 393248 | tf_op jit(solution)/shard_map/all_to_all | solution.py:358
  29.4 0.8 chain.1
  30.2 4.3 %all-to-all-start.1 = ((bf16[32,16,256]{2,1,0:T(8,128)(2,1)}), bf16[32,16,256]{2,1,0:T(8,128)(2,1)S(1)}, u32[]{:S(2)}, u32[]{:S(2)}) async-start(bf16[32,16,256]{2,1,0:T(8,128)(2,1)} %chain.1), calls=%async_computation.1 | async-start | bytes 524288 | tf_op jit(solution)/shard_map/all_to_all | solution.py:361
  34.5 0.0 copy-start
  34.5 0.0 copy-start.1
  34.6 6.9 %inside1.1 = (bf16[2048,256]{1,0:T(8,128)(2,1)}, bf16[2048,256]{1,0:T(8,128)(2,1)}) custom-call(s32[1]{0:T(128)} %bitcast.where_ref, bf16[2048,512]{1,0:T(8,128)(2,1)} %q_ref.5, bf16[2048,512]{1,0:T(8,128)(2,1)} %k_ref.5, bf16[2048,512]{1,0:T(8,128)(2,1)} %v_ref.5, bf16[2048,512]{1,0:T(8,128)(2,1)} %g_ref.5, f32[8,2048]{1,0:T(8,128)} %ld_ref.7), custom_call_target="tpu_custom_call" | custom-call | flops 2147483648 | bytes 6291456 | tf_op jit(solution)/shard_map/inside1/pallas_call | solution.py:183
  41.5 2.8 %all-to-all-done.1 = bf16[32,16,256]{2,1,0:T(8,128)(2,1)S(1)} async-done(((bf16[32,16,256]{2,1,0:T(8,128)(2,1)}), bf16[32,16,256]{2,1,0:T(8,128)(2,1)S(1)}, u32[]{:S(2)}, u32[]{:S(2)}) %all-to-all-start.1) | async-done | bytes 262176 | tf_op jit(solution)/shard_map/all_to_all | solution.py:361
  44.3 0.0 copy-done
  44.3 0.0 copy-done.1
  44.3 17.7 %finish.1 = (bf16[2048,512]{1,0:T(8,128)(2,1)}, bf16[2048,512]{1,0:T(8,128)(2,1)}, bf16[4,8,128,512]{3,2,1,0:T(8,128)(2,1)S(1)}) custom-call(s32[1]{0:T(128)} %bitcast.where_ref, bf16[2,256,256]{2,1,0:T(8,128)(2,1)S(1)} %bitcast.2, f32[4,2,256,256]{3,2,1,0:T(8,128)} %get-tuple-element.21.state_ref, bf16[2048,512]{1,0:T(8,128)(2,1)} %k_ref.5, ...), custom_call_target="tpu_custom_call" | custom-call | flops 9663676416 | bytes 16777216 | tf_op jit(solution)/shard_map/finish/pallas_call | solution.py:268
  62.1 29.4 %all_to_all.20.parts_ref = bf16[4,8,128,512]{3,2,1,0:T(8,128)(2,1)S(1)} all-to-all(bf16[4,8,128,512]{3,2,1,0:T(8,128)(2,1)S(1)} %get-tuple-element.28), channel_id=1, replica_groups={{0,32,64,96},{2,34,66,98},{4,36,68,100},{6,38,70,102},{8,40,72,104},{10..., dimensions={0} | all-to-all | bytes 8388608 | tf_op jit(solution)/shard_map/all_to_all | solution.py:349
  91.5 0.5 near.1
  92.0 21.9 %all_to_all.21.parts_ref = bf16[8,128,512]{2,1,0:T(8,128)(2,1)S(1)} all-to-all(bf16[8,128,512]{2,1,0:T(8,128)(2,1)S(1)} %near.1), channel_id=1, replica_groups={{0,4,8,12,16,20,24,28},{2,6,10,14,18,22,26,30},{32,36,40,44,48,52,56,60..., dimensions={0} | all-to-all | bytes 2097152 | tf_op jit(solution)/shard_map/all_to_all | solution.py:349
  113.9 0.9 far.1
Async XLA Ops:
  6.6 22.8 %all-to-all-start = ((bf16[32,16,384]{2,1,0:T(8,128)(2,1)}), bf16[32,16,384]{2,1,0:T(8,128)(2,1)S(1)}, u32[]{:S(2)}, u32[]{:S(2)}) async-start(bf16[32,16,384]{2,1,0:T(8,128)(2,1)} %get-tuple-element.16), calls=%async_computation | async-start | bytes 786432 | tf_op jit(solution)/shard_map/all_to_all | solution.py:358
  30.2 14.1 %all-to-all-start.1 = ((bf16[32,16,256]{2,1,0:T(8,128)(2,1)}), bf16[32,16,256]{2,1,0:T(8,128)(2,1)S(1)}, u32[]{:S(2)}, u32[]{:S(2)}) async-start(bf16[32,16,256]{2,1,0:T(8,128)(2,1)} %chain.1), calls=%async_computation.1 | async-start | bytes 524288 | tf_op jit(solution)/shard_map/all_to_all | solution.py:361
  34.5 9.8 %copy-start = (f32[8,2048]{1,0:T(8,128)S(1)}, f32[8,2048]{1,0:T(8,128)}, u32[]{:S(2)}) copy-start(f32[8,2048]{1,0:T(8,128)} %ld_ref.7) | copy-start | bytes 196612
  34.5 9.8 %copy-start.1 = (bf16[2048,256]{1,0:T(8,128)(2,1)S(1)}, bf16[2048,256]{1,0:T(8,128)(2,1)}, u32[]{:S(2)}) copy-start(bf16[2048,256]{1,0:T(8,128)(2,1)} %get-tuple-element.22.refs_0_) | copy-start | bytes 3145732

commit v4 on v3

--- a/solution.py
+++ b/solution.py
@@ -58,7 +58,7 @@
         passed[...] = jnp.zeros_like(passed)
 
     cum = cumulate(own_rows(ld_ref[...], where_ref[0] * heads, heads))
-    decay = (SCALE * jnp.exp(cum)).T
+    decay = SCALE * jnp.exp(cum)
     before = passed[:, 0:1]
     sums = [total[h] for h in range(heads)]
     for c in range(state_ref.shape[0]):
@@ -66,8 +66,8 @@
         kept = jnp.exp(before)
         for h in range(heads):
             cols = slice(h * DH, (h + 1) * DH)
-            weighted = (q_ref[rows, cols].astype(F32) * decay[rows, h : h + 1]).astype(BF16)
-            state = dot_tt(weighted, g_ref[rows, cols])
+            weighted = (q_ref[rows, cols].T.astype(F32) * decay[h : h + 1, rows]).astype(BF16)
+            state = dot_nn(weighted, g_ref[rows, cols])
             state_ref[c, h] = state
             sums[h] = sums[h] + kept[h : h + 1, :] * state
         before = before + cum[:, (c + 1) * BLOCK - 1 : (c + 1) * BLOCK]

time: 115 us -> 114 us (level)
  no operation moved by 1% of the time
where the time goes in v4:
time: 114 us
  blocking collectives  51.3 us (45%)
  Pallas kernels  38.5 us (34%)
  starting transfers between devices  15.6 us (14%)
  waiting for transfers between devices  7.76 us (7%)
    all_to_all x2, blocking collectives, exchanged(): lax.all_to_all(pieces, EVERY, 0, 0, axis_index_groups=groups_of(*axes_of_...  51.3 us
    pallas_call x1, Pallas kernels, finish(): pl.pallas_call(functools.partial(finish_kernel, heads, steps), grid_spec=...  17.7 us
    pallas_call x2, Pallas kernels, inside(): pl.pallas_call(functools.partial(inside_kernel, heads, head), grid_spec=p...  13.5 us
    all_to_all x1, starting transfers between devices, shards(): arrived = lax.all_to_all(message, SEQ, 0, 0, tiled=True)  11.3 us
    pallas_call x1, Pallas kernels, block_states(): pl.pallas_call(functools.partial(states_kernel, heads), grid_spec=pltpu.P...  5.15 us
    all_to_all x1, waiting for transfers between devices, shards(): arrived = lax.all_to_all(message, SEQ, 0, 0, tiled=True)  4.93 us
    all_to_all x1, starting transfers between devices, shards(): carried = lax.all_to_all(chain(arrived), SEQ, 0, 0, tiled=True)  4.3 us
    all_to_all x1, waiting for transfers between devices, shards(): carried = lax.all_to_all(chain(arrived), SEQ, 0, 0, tiled=True)  2.83 us
  transfers between devices with their start and end apart: 2, of which 2 were waited for; matrix products, arithmetic and copies ran while one was open for 0% of the time, Pallas kernels for 12%

profile of v4, /device:TPU:1, one launch (start us, length us, event | category | flops | bytes accessed | tf_op | source)
XLA Modules:
  0.0 113.9 jit_solution(11918425996773449446)
XLA Ops:
  0.6 5.1 %states.1 = (f32[4,2,256,256]{3,2,1,0:T(8,128)}, bf16[32,16,384]{2,1,0:T(8,128)(2,1)}) custom-call(s32[1]{0:T(128)} %bitcast.where_ref, bf16[2048,512]{1,0:T(8,128)(2,1)} %q_ref.5, bf16[2048,512]{1,0:T(8,128)(2,1)} %g_ref.5, f32[8,2048]{1,0:T(8,128)} %ld_ref.7), custom_call_target="tpu_custom_call" | custom-call | flops 536870912 | bytes 6291456 | tf_op jit(solution)/shard_map/states/pallas_call | solution.py:101
  5.8 11.3 %all-to-all-start = ((bf16[32,16,384]{2,1,0:T(8,128)(2,1)}), bf16[32,16,384]{2,1,0:T(8,128)(2,1)S(1)}, u32[]{:S(2)}, u32[]{:S(2)}) async-start(bf16[32,16,384]{2,1,0:T(8,128)(2,1)} %get-tuple-element.16), calls=%async_computation | async-start | bytes 786432 | tf_op jit(solution)/shard_map/all_to_all | solution.py:358
  17.1 6.5 %inside0.1 = (bf16[2048,256]{1,0:T(8,128)(2,1)}, bf16[2048,256]{1,0:T(8,128)(2,1)}) custom-call(s32[1]{0:T(128)} %bitcast.where_ref, bf16[2048,512]{1,0:T(8,128)(2,1)} %q_ref.5, bf16[2048,512]{1,0:T(8,128)(2,1)} %k_ref.5, bf16[2048,512]{1,0:T(8,128)(2,1)} %v_ref.5, bf16[2048,512]{1,0:T(8,128)(2,1)} %g_ref.5, f32[8,2048]{1,0:T(8,128)} %ld_ref.7), custom_call_target="tpu_custom_call" | custom-call | flops 2147483648 | bytes 6291456 | tf_op jit(solution)/shard_map/inside0/pallas_call | solution.py:183
  23.7 4.9 %all-to-all-done.message_ref = bf16[32,16,384]{2,1,0:T(8,128)(2,1)S(1)} async-done(((bf16[32,16,384]{2,1,0:T(8,128)(2,1)}), bf16[32,16,384]{2,1,0:T(8,128)(2,1)S(1)}, u32[]{:S(2)}, u32[]{:S(2)}) %all-to-all-start) | async-done | bytes 393248 | tf_op jit(solution)/shard_map/all_to_all | solution.py:358
  28.6 0.8 chain.1
  29.4 4.3 %all-to-all-start.1 = ((bf16[32,16,256]{2,1,0:T(8,128)(2,1)}), bf16[32,16,256]{2,1,0:T(8,128)(2,1)S(1)}, u32[]{:S(2)}, u32[]{:S(2)}) async-start(bf16[32,16,256]{2,1,0:T(8,128)(2,1)} %chain.1), calls=%async_computation.1 | async-start | bytes 524288 | tf_op jit(solution)/shard_map/all_to_all | solution.py:361
  33.7 0.0 copy-start
  33.7 0.0 copy-start.1
  33.7 6.9 %inside1.1 = (bf16[2048,256]{1,0:T(8,128)(2,1)}, bf16[2048,256]{1,0:T(8,128)(2,1)}) custom-call(s32[1]{0:T(128)} %bitcast.where_ref, bf16[2048,512]{1,0:T(8,128)(2,1)} %q_ref.5, bf16[2048,512]{1,0:T(8,128)(2,1)} %k_ref.5, bf16[2048,512]{1,0:T(8,128)(2,1)} %v_ref.5, bf16[2048,512]{1,0:T(8,128)(2,1)} %g_ref.5, f32[8,2048]{1,0:T(8,128)} %ld_ref.7), custom_call_target="tpu_custom_call" | custom-call | flops 2147483648 | bytes 6291456 | tf_op jit(solution)/shard_map/inside1/pallas_call | solution.py:183
  40.7 2.8 %all-to-all-done.1 = bf16[32,16,256]{2,1,0:T(8,128)(2,1)S(1)} async-done(((bf16[32,16,256]{2,1,0:T(8,128)(2,1)}), bf16[32,16,256]{2,1,0:T(8,128)(2,1)S(1)}, u32[]{:S(2)}, u32[]{:S(2)}) %all-to-all-start.1) | async-done | bytes 262176 | tf_op jit(solution)/shard_map/all_to_all | solution.py:361
  43.5 0.0 copy-done
  43.5 0.0 copy-done.1
  43.5 17.7 %finish.1 = (bf16[2048,512]{1,0:T(8,128)(2,1)}, bf16[2048,512]{1,0:T(8,128)(2,1)}, bf16[4,8,128,512]{3,2,1,0:T(8,128)(2,1)S(1)}) custom-call(s32[1]{0:T(128)} %bitcast.where_ref, bf16[2,256,256]{2,1,0:T(8,128)(2,1)S(1)} %bitcast.2, f32[4,2,256,256]{3,2,1,0:T(8,128)} %get-tuple-element.21.state_ref, bf16[2048,512]{1,0:T(8,128)(2,1)} %k_ref.5, ...), custom_call_target="tpu_custom_call" | custom-call | flops 9663676416 | bytes 16777216 | tf_op jit(solution)/shard_map/finish/pallas_call | solution.py:268
  61.2 29.4 %all_to_all.20.parts_ref = bf16[4,8,128,512]{3,2,1,0:T(8,128)(2,1)S(1)} all-to-all(bf16[4,8,128,512]{3,2,1,0:T(8,128)(2,1)S(1)} %get-tuple-element.28), channel_id=1, replica_groups={{0,32,64,96},{2,34,66,98},{4,36,68,100},{6,38,70,102},{8,40,72,104},{10..., dimensions={0} | all-to-all | bytes 8388608 | tf_op jit(solution)/shard_map/all_to_all | solution.py:349
  90.7 0.5 near.1
  91.2 21.9 %all_to_all.21.parts_ref = bf16[8,128,512]{2,1,0:T(8,128)(2,1)S(1)} all-to-all(bf16[8,128,512]{2,1,0:T(8,128)(2,1)S(1)} %near.1), channel_id=1, replica_groups={{0,4,8,12,16,20,24,28},{2,6,10,14,18,22,26,30},{32,36,40,44,48,52,56,60..., dimensions={0} | all-to-all | bytes 2097152 | tf_op jit(solution)/shard_map/all_to_all | solution.py:349
  113.1 0.9 far.1
Async XLA Ops:
  5.8 22.8 %all-to-all-start = ((bf16[32,16,384]{2,1,0:T(8,128)(2,1)}), bf16[32,16,384]{2,1,0:T(8,128)(2,1)S(1)}, u32[]{:S(2)}, u32[]{:S(2)}) async-start(bf16[32,16,384]{2,1,0:T(8,128)(2,1)} %get-tuple-element.16), calls=%async_computation | async-start | bytes 786432 | tf_op jit(solution)/shard_map/all_to_all | solution.py:358
  29.4 14.1 %all-to-all-start.1 = ((bf16[32,16,256]{2,1,0:T(8,128)(2,1)}), bf16[32,16,256]{2,1,0:T(8,128)(2,1)S(1)}, u32[]{:S(2)}, u32[]{:S(2)}) async-start(bf16[32,16,256]{2,1,0:T(8,128)(2,1)} %chain.1), calls=%async_computation.1 | async-start | bytes 524288 | tf_op jit(solution)/shard_map/all_to_all | solution.py:361
  33.7 9.8 %copy-start = (f32[8,2048]{1,0:T(8,128)S(1)}, f32[8,2048]{1,0:T(8,128)}, u32[]{:S(2)}) copy-start(f32[8,2048]{1,0:T(8,128)} %ld_ref.7) | copy-start | bytes 196612
  33.7 9.8 %copy-start.1 = (bf16[2048,256]{1,0:T(8,128)(2,1)S(1)}, bf16[2048,256]{1,0:T(8,128)(2,1)}, u32[]{:S(2)}) copy-start(bf16[2048,256]{1,0:T(8,128)(2,1)} %get-tuple-element.22.refs_0_) | copy-start | bytes 3145732
